TPU v7x, 256 devices: a whole 4x4x8 slice. The times are simulated.
256 devices in a mesh: row: 4 (over z_hi, core), col: 16 (over z_lo, y), layer: 4 (over x).
Axes of the slice: x: 4, y: 4, z: 8 (z_hi: 2, z_lo: 4; z = z_hi * 4 + z_lo), core: 2. Of those that a mesh axis runs over, the one named last changes fastest.
Arguments:
- amplitudes: float32 [2016, 73536], P('row', ('layer', 'col')), may hold values from -6 to 6
- integrals: float32 [73536, 768], P(('layer', 'col'), 'row'), may hold values from -0.0625 to 0.0625
- occ_energy: float32 [64], replicated, may hold values from -2 to -0.5
- vir_energy: float32 [384], replicated, may hold values from 0.2 to 3
Outputs:
- ladder: float32 [2016, 768], P('col', ('row', 'layer'))
- amplitude_step: float32 [2016, 768], P('col', ('row', 'layer'))
All inputs are finite; a program needn't handle non-finite values.
Results may differ from a plain program's by a relative error of at most 0.00007.
Values sent between devices are 32-bit elements; how exact they have to be, the bound alone decides.
A program may use at most 64 MiB of HBM per device.

v0:
```python
import jax
import jax.numpy as jnp
import numpy as np
from jax import lax
from jax.sharding import PartitionSpec as P


def in_blocks(array, dim, count):
    shape = array.shape
    parts = array.reshape(*shape[:dim], count, shape[dim] // count, *shape[dim + 1 :])
    return jnp.moveaxis(parts, dim, 0)


def summed_on_arrival(array, axis, dim):
    count = lax.axis_size(axis)
    parts = lax.all_to_all(in_blocks(array, dim, count), axis, 0, 0, tiled=True)
    return jnp.sum(parts, axis=0)


def lookup(indices, values_table):
    positions = jnp.arange(values_table.shape[0], dtype=jnp.int32)
    picked = jnp.where(indices[:, None] == positions[None, :], values_table[None, :], 0.0)
    return jnp.sum(picked, axis=1)


def owner_blocks(partial_sum):
    col_count = lax.axis_size("col")
    layer_count = lax.axis_size("layer")
    pair_rows = partial_sum.shape[0] // col_count
    slab_cols = partial_sum.shape[1] // layer_count
    blocks = partial_sum.reshape(col_count, pair_rows, layer_count, slab_cols)
    return blocks.transpose(0, 2, 1, 3).reshape(col_count * layer_count * pair_rows, slab_cols)


def shards(amplitudes, integrals, occ_energy, vir_energy):
    partial_rows = jnp.dot(
        amplitudes,
        lax.all_gather(integrals, "row", axis=1, tiled=True),
        precision=lax.Precision.HIGHEST,
        preferred_element_type=jnp.float32,
    )
    partial_sum = lax.all_to_all(partial_rows, "row", split_axis=1, concat_axis=0, tiled=True)
    ladder = summed_on_arrival(owner_blocks(partial_sum), ("col", "layer"), 0)
    pair_rows = ladder.shape[0]
    slab_cols = ladder.shape[1]
    occupied = occ_energy.shape[0]
    virtuals = vir_energy.shape[0]
    first_np, second_np = np.triu_indices(occupied, 1)
    ij_start = lax.axis_index("col") * pair_rows
    ab_start = (
        lax.axis_index("row") * lax.axis_size("layer") + lax.axis_index("layer")
    ) * slab_cols
    first_index = lax.dynamic_slice_in_dim(
        jnp.asarray(first_np, dtype=jnp.int32), ij_start, pair_rows
    )
    second_index = lax.dynamic_slice_in_dim(
        jnp.asarray(second_np, dtype=jnp.int32), ij_start, pair_rows
    )
    pair_sum = lookup(first_index, occ_energy) + lookup(second_index, occ_energy)
    ab_index = ab_start + jnp.arange(slab_cols, dtype=jnp.int32)
    vir_sum = lookup(ab_index // virtuals, vir_energy) + lookup(ab_index % virtuals, vir_energy)
    denominator = pair_sum[:, None] - vir_sum[None, :]
    return (ladder, ladder / denominator)


def solution(mesh):
    in_specs = (P("row", ("layer", "col")), P(("layer", "col"), "row"), P(), P())
    out_specs = (P("col", ("row", "layer")), P("col", ("row", "layer")))
    return jax.shard_map(shards, mesh=mesh, in_specs=in_specs, out_specs=out_specs, check_vma=False)
```

profile of v0, /device:TPU:2, one launch (start us, length us, event | category | flops | bytes accessed | tf_op | source)
XLA Modules:
  0.0 188.2 jit_solution(8743574905029735897)
XLA Ops:
  7.2 0.0 copy-start
  7.2 0.0 all-gather.2.cloned.1.call-start
  7.2 0.7 all-gather.2.cloned.1.call-update
  7.9 64.1 %all-gather.2.cloned.1.call-done = f32[1149,768]{0,1:T(8,128)} async-done(((f32[1149,192]{0,1:T(8,128)}), f32[1149,768]{0,1:T(8,128)}) %all-gather.2.cloned.1.call-update) | async-done | bytes 3529744 | tf_op jit(solution)/shard_map/all_gather | solution.py:38
  72.0 0.0 copy-done
  72.0 8.3 %fusion.1 = f32[504,768]{0,1:T(8,128)S(1)} fusion(f32[504,1149]{1,0:T(8,128)S(1)} %copy-done, f32[1149,768]{0,1:T(8,128)} %all-gather.2.cloned.1.call-done), kind=kOutput, calls=%fused_computation.13 | convolution fusion | flops 5336948736 | bytes 7394400 | tf_op jit(solution)/shard_map/dot_general | solution.py:36
  80.3 35.7 %all_to_all.21 = f32[504,4,192]{0,2,1:T(8,128)S(1)} all-to-all(f32[504,4,192]{0,2,1:T(8,128)S(1)} %bitcast.11), channel_id=1, replica_groups=mesh['row'=4,'col'=16,'layer'=4] {'row'}, dimensions={1} | all-to-all | bytes 3096576 | tf_op jit(solution)/shard_map/all_to_all | solution.py:42
  116.0 2.2 %copy.12 = f32[4,504,192]{1,0,2:T(4,128)} copy(f32[4,504,192]{1,2,0:T(8,128)S(1)} %bitcast.9) | data formatting | bytes 3096576 | tf_op jit(solution)/shard_map/all_to_all | solution.py:42
  118.2 2.9 %reshape.43 = f32[16,126,4,48]{1,0,3,2:T(8,128)} reshape(f32[4,504,192]{1,0,2:T(4,128)} %copy.12) | data formatting | bytes 3096576 | tf_op jit(solution)/shard_map/reshape | solution.py:31
  121.1 3.1 %copy.13 = f32[16,4,126,48]{2,3,1,0:T(8,128)} copy(f32[16,4,126,48]{2,0,3,1:T(8,128)} %bitcast.10) | data formatting | bytes 3096576 | tf_op jit(solution)/shard_map/transpose | solution.py:32
  124.2 0.0 copy-start.2
  124.2 0.0 copy-start.3
  124.2 16.2 %all-to-all-start.1 = ((f32[64,126,48]{1,2,0:T(8,128)}), f32[64,126,48]{1,2,0:T(8,128)}, u32[]{:S(2)}, u32[]{:S(2)}) async-start(f32[64,126,48]{1,2,0:T(8,128)} %bitcast.8), calls=%async_computation.1 | async-start | bytes 3145728 | tf_op jit(solution)/shard_map/all_to_all | solution.py:16
  140.4 0.8 dynamic_slice.7
  141.2 0.8 dynamic_slice.6
  142.0 0.0 copy-done.2
  142.0 0.2 select_reduce_fusion
  142.2 0.0 copy-done.3
  142.2 0.1 select_reduce_fusion.2
  142.3 36.7 %all-to-all-done.1 = f32[64,126,48]{1,2,0:T(8,128)} async-done(((f32[64,126,48]{1,2,0:T(8,128)}), f32[64,126,48]{1,2,0:T(8,128)}, u32[]{:S(2)}, u32[]{:S(2)}) %all-to-all-start.1) | async-done | bytes 1548320 | tf_op jit(solution)/shard_map/all_to_all | solution.py:16
  179.1 1.6 reduce_sum.45
  180.6 0.0 copy-start.1
  180.6 0.7 subtract_divide_fusion
  181.3 0.0 copy-done.1
  (3 shorter events, 0.0 us)
Async XLA Ops:
  7.2 64.9 %copy-start = (f32[504,1149]{1,0:T(8,128)S(1)}, f32[504,1149]{1,0:T(8,128)}, u32[]{:S(2)}) copy-start(f32[504,1149]{1,0:T(8,128)} %param.6) | copy-start | bytes 6949156
  7.2 64.8 %all-gather.2.cloned.1.call-start = ((), (), s32[]{:S(2)}) async-start(), calls=%async_computation.2 | async-start | bytes 4423680 | tf_op jit(solution)/shard_map/all_gather | solution.py:38
  124.2 17.8 %copy-start.2 = (f32[384]{0:T(512)S(1)}, f32[384]{0:T(512)}, u32[]{:S(2)}) copy-start(f32[384]{0:T(512)} %param.9) | copy-start | bytes 4612
  124.2 18.0 %copy-start.3 = (f32[64]{0:T(128)S(1)}, f32[64]{0:T(128)}, u32[]{:S(2)}) copy-start(f32[64]{0:T(128)} %param.8) | copy-start | bytes 772
  124.2 54.9 %all-to-all-start.1 = ((f32[64,126,48]{1,2,0:T(8,128)}), f32[64,126,48]{1,2,0:T(8,128)}, u32[]{:S(2)}, u32[]{:S(2)}) async-start(f32[64,126,48]{1,2,0:T(8,128)} %bitcast.8), calls=%async_computation.1 | async-start | bytes 3145728 | tf_op jit(solution)/shard_map/all_to_all | solution.py:16
  180.6 0.7 copy-start.1
Sparse Core Ops, SparseCore 0:
  9.8 62.1 all-gather.1
where the time goes:
time: 189 us; the launch traced here: 188 us
  waiting for transfers between devices  102 us (54%)
  blocking collectives  35.7 us (19%)
  starting transfers between devices  16.3 us (9%)
  between operations  14.1 us (7%)
  local copies, waits for them, and re-layouts  9.7 us (5%)
  matrix products  8.3 us (4%)
  other arithmetic  2.55 us (1%)
    all_gather x1, waiting for transfers between devices, shards(): lax.all_gather(integrals, 'row', axis=1, tiled=True)  64.1 us
    all_to_all x1, waiting for transfers between devices, summed_on_arrival(): parts = lax.all_to_all(in_blocks(array, dim, count), axis, 0, 0, tiled=True)  36.7 us
    all_to_all x1, blocking collectives, shards(): lax.all_to_all(partial_rows, 'row', split_axis=1, concat_axis=0, tiled=True)  35.7 us
    all_to_all x1, starting transfers between devices, summed_on_arrival(): parts = lax.all_to_all(in_blocks(array, dim, count), axis, 0, 0, tiled=True)  16.2 us
    dot_general x1, matrix products, shards(): jnp.dot(amplitudes, lax.all_gather(integrals, 'row', axis=1, tiled=True),...  8.3 us
  transfers between devices with their start and end apart: 2, of which 2 were waited for; matrix products, arithmetic and copies ran while one was open for 1% of the time, Pallas kernels for 0%

commit v1 on v0

--- a/solution.py
+++ b/solution.py
@@ -35,7 +35,15 @@
 def shards(amplitudes, integrals, occ_energy, vir_energy):
     partial_rows = jnp.dot(
         amplitudes,
-        lax.all_gather(integrals, "row", axis=1, tiled=True),
+        jnp.concatenate(
+            jax.lax.all_to_all(
+                jnp.stack(jax.lax.axis_size("row") * [integrals], 0),
+                split_axis=0,
+                concat_axis=0,
+                axis_name="row",
+            ),
+            1,
+        ),
         precision=lax.Precision.HIGHEST,
         preferred_element_type=jnp.float32,
     )

time: 189 us -> 201 us (1.063)
  blocking collectives: 35.7 us -> 133 us
  waiting for transfers between devices: 102 us -> 36.7 us
  between operations: 14.1 us -> 0.7 us
  starting transfers between devices: 16.3 us -> 9.95 us
    all_to_all x0 -> x1, blocking collectives: none -> 90.7 us  [shards(): jax.lax.all_to_all(jnp.stack(jax.lax.axis_size('row') * [integrals], 0),...]
    all_gather x1 -> x0, waiting for transfers between devices: 64.1 us -> none  [shards(): lax.all_gather(integrals, 'row', axis=1, tiled=True)]
    all_to_all x1, blocking collectives: 35.7 us -> 42.6 us  [shards(): lax.all_to_all(partial_rows, 'row', split_axis=1, concat_axis=0, tiled=True)]
    all_to_all x1, starting transfers between devices: 16.2 us -> 9.95 us  [summed_on_arrival(): parts = lax.all_to_all(in_blocks(array, dim, count), axis, 0, 0, tiled=True)]
  transfers between devices with their start and end apart: 2 -> 1, of which waited for: 2 -> 1; matrix products, arithmetic and copies ran while one was open for 1% -> 1% of each run, Pallas kernels for 0% -> 0%
where the time goes in v1:
time: 201 us
  blocking collectives  133 us (66%)
  waiting for transfers between devices  36.7 us (18%)
  local copies, waits for them, and re-layouts  11.2 us (6%)
  starting transfers between devices  9.95 us (5%)
  matrix products  6.4 us (3%)
  other arithmetic  2.55 us (1%)
    all_to_all x1, blocking collectives, shards(): jax.lax.all_to_all(jnp.stack(jax.lax.axis_size('row') * [integrals], 0),...  90.7 us
    all_to_all x1, blocking collectives, shards(): lax.all_to_all(partial_rows, 'row', split_axis=1, concat_axis=0, tiled=True)  42.6 us
    all_to_all x1, waiting for transfers between devices, summed_on_arrival(): parts = lax.all_to_all(in_blocks(array, dim, count), axis, 0, 0, tiled=True)  36.7 us
    all_to_all x1, starting transfers between devices, summed_on_arrival(): parts = lax.all_to_all(in_blocks(array, dim, count), axis, 0, 0, tiled=True)  9.95 us
    dot_general x1, matrix products, shards(): jnp.dot(amplitudes, jnp.concatenate(jax.lax.all_to_all(jnp.stack(jax.lax....  6.4 us
  transfers between devices with their start and end apart: 1, of which 1 were waited for; matrix products, arithmetic and copies ran while one was open for 1% of the time, Pallas kernels for 0%

profile of v1, /device:TPU:2, one launch (start us, length us, event | category | flops | bytes accessed | tf_op | source)
XLA Modules:
  0.0 200.9 jit_solution(1172027387834108615)
XLA Ops:
  0.6 0.0 copy-start
  0.6 1.5 stack.2
  2.2 90.7 %all_to_all.23 = f32[4,1149,192]{1,2,0:T(8,128)S(1)} all-to-all(f32[4,1149,192]{1,2,0:T(8,128)S(1)} %stack.2), channel_id=1, replica_groups=mesh['row'=4,'col'=16,'layer'=4] {'row'}, dimensions={0} | all-to-all | bytes 7059456 | tf_op jit(solution)/shard_map/all_to_all | solution.py:39
  92.8 0.0 copy-done
  92.8 6.4 %fusion = f32[504,4,192]{0,2,1:T(8,128)S(1)} fusion(f32[4,1149,192]{1,2,0:T(8,128)S(1)} %all_to_all.23, f32[504,1149]{1,0:T(8,128)S(1)} %copy-done), kind=kOutput, calls=%fused_computation | convolution fusion | flops 5336948736 | bytes 7394400 | tf_op jit(solution)/shard_map/dot_general | solution.py:36
  99.3 42.6 %all_to_all.24 = f32[504,4,192]{0,2,1:T(8,128)S(1)} all-to-all(f32[504,4,192]{0,2,1:T(8,128)S(1)} %fusion), channel_id=1, replica_groups=mesh['row'=4,'col'=16,'layer'=4] {'row'}, dimensions={1} | all-to-all | bytes 3096576 | tf_op jit(solution)/shard_map/all_to_all | solution.py:50
  141.9 2.2 %copy.10 = f32[4,504,192]{1,0,2:T(4,128)} copy(f32[4,504,192]{1,2,0:T(8,128)S(1)} %bitcast.18) | data formatting | bytes 3096576 | tf_op jit(solution)/shard_map/all_to_all | solution.py:50
  144.1 2.9 %reshape.54 = f32[16,126,4,48]{1,0,3,2:T(8,128)} reshape(f32[4,504,192]{1,0,2:T(4,128)} %copy.10) | data formatting | bytes 3096576 | tf_op jit(solution)/shard_map/reshape | solution.py:31
  147.0 3.1 %copy.11 = f32[16,4,126,48]{2,3,1,0:T(8,128)} copy(f32[16,4,126,48]{2,0,3,1:T(8,128)} %bitcast.19) | data formatting | bytes 3096576 | tf_op jit(solution)/shard_map/transpose | solution.py:32
  150.0 0.0 copy-start.2
  150.0 0.0 copy-start.3
  150.0 9.9 %all-to-all-start.2 = ((f32[64,126,48]{1,2,0:T(8,128)}), f32[64,126,48]{1,2,0:T(8,128)}, u32[]{:S(2)}, u32[]{:S(2)}) async-start(f32[64,126,48]{1,2,0:T(8,128)} %bitcast.17), calls=%async_computation.2 | async-start | bytes 3145728 | tf_op jit(solution)/shard_map/all_to_all | solution.py:16
  160.0 0.8 dynamic_slice.7
  160.8 0.8 dynamic_slice.6
  161.6 0.0 copy-done.2
  161.6 0.2 select_reduce_fusion
  161.8 0.0 copy-done.3
  161.8 0.1 select_reduce_fusion.2
  161.9 36.7 %all-to-all-done.2 = f32[64,126,48]{1,2,0:T(8,128)} async-done(((f32[64,126,48]{1,2,0:T(8,128)}), f32[64,126,48]{1,2,0:T(8,128)}, u32[]{:S(2)}, u32[]{:S(2)}) %all-to-all-start.2) | async-done | bytes 1548320 | tf_op jit(solution)/shard_map/all_to_all | solution.py:16
  198.6 1.6 reduce_sum.45
  200.2 0.0 copy-start.1
  200.2 0.7 subtract_divide_fusion
  200.9 0.0 copy-done.1
  (3 shorter events, 0.0 us)
Async XLA Ops:
  0.6 92.2 %copy-start = (f32[504,1149]{1,0:T(8,128)S(1)}, f32[504,1149]{1,0:T(8,128)}, u32[]{:S(2)}) copy-start(f32[504,1149]{1,0:T(8,128)} %param.6) | copy-start | bytes 6949156
  150.0 11.5 %copy-start.2 = (f32[384]{0:T(512)S(1)}, f32[384]{0:T(512)}, u32[]{:S(2)}) copy-start(f32[384]{0:T(512)} %param.9) | copy-start | bytes 4612
  150.0 11.7 %copy-start.3 = (f32[64]{0:T(128)S(1)}, f32[64]{0:T(128)}, u32[]{:S(2)}) copy-start(f32[64]{0:T(128)} %param.8) | copy-start | bytes 772
  150.0 48.6 %all-to-all-start.2 = ((f32[64,126,48]{1,2,0:T(8,128)}), f32[64,126,48]{1,2,0:T(8,128)}, u32[]{:S(2)}, u32[]{:S(2)}) async-start(f32[64,126,48]{1,2,0:T(8,128)} %bitcast.17), calls=%async_computation.2 | async-start | bytes 3145728 | tf_op jit(solution)/shard_map/all_to_all | solution.py:16
  200.2 0.7 copy-start.1
